TPU v7x, 32 devices: a whole 2x2x4 slice. The times are simulated.
32 devices in a mesh: gz: 2 (over x), gy: 4 (over y, core), gx: 4 (over z).
Axes of the slice: x: 2, y: 2, z: 4, core: 2. Of those that a mesh axis runs over, the one named last changes fastest.
Arguments:
- density: float32 [32, 64, 256], P('gx', 'gy', 'gz'), may hold values from 0.05 to 0.95
- spread: float32 [32, 64, 256], P('gx', 'gy', 'gz'), may hold values from 0.05 to 0.3
- sensitivities: float32 [9, 32, 64, 256], P(None, 'gx', 'gy', 'gz'), may hold values from -180 to 180, as said below
- violation: float32 [9], replicated, may hold values from -0.05 to 0.15
- multipliers_start: float32 [9], replicated, may hold values from 0.1 to 10
Outputs:
- new_density: float32 [32, 64, 256], P('gx', 'gy', 'gz')
- multipliers: float32 [9], replicated
Inputs may be any that keep to these rules, and one draw needn't show every extreme that they name: `sensitivities`: Real-valued, independent from voxel to voxel.
All inputs are finite; a program needn't handle non-finite values.
Results may differ from a plain program's by a relative error of at most 0.0003.
Values sent between devices are 32-bit elements; how exact they have to be, the bound alone decides.
A program may use at most 64 MiB of HBM per device.

v0:
```python
import math
import jax
import jax.numpy as jnp
from jax import lax
from jax.sharding import PartitionSpec as P

FIELDS = 9
ITERS = 3
RADIUS = 3.0
RAA = 1e-05
MOVE = 0.9
REG = 0.001
FLOOR = 0.2


def padded_2(block, sides, width):
    for axis, dim in sides:
        count = lax.axis_size(axis)
        forward = [(i, i + 1) for i in range(count - 1)]
        backward = [(target, source) for source, target in forward]
        low = lax.ppermute(
            lax.slice_in_dim(block, block.shape[dim] - width, None, axis=dim), axis, forward
        )
        high = lax.ppermute(lax.slice_in_dim(block, 0, width, axis=dim), axis, backward)
        block = jnp.concatenate([low, block, high], axis=dim)
    return block


def smooth(padded, nx, ny, nz):
    total = None
    for a in (-1, 0, 1):
        for b in (-1, 0, 1):
            for c in (-1, 0, 1):
                weight = RADIUS - math.sqrt(a * a + b * b + c * c)
                piece = padded[..., 1 + a : 1 + a + nx, 1 + b : 1 + b + ny, 1 + c : 1 + c + nz]
                total = weight * piece if total is None else total + weight * piece
    return total


def inside(index, extent, count):
    first = (index > 0).astype(jnp.float32)
    last = (index < extent - 1).astype(jnp.float32)
    return jnp.concatenate([first[None], jnp.ones((count,), jnp.float32), last[None]])


def totals(gradient_part, schur_part):
    return lax.psum((gradient_part, schur_part), ("gz", "gy", "gx"))


def shards(density, spread, sensitivities, violation, multipliers_start):
    nx, ny, nz = density.shape
    padded = padded_2(sensitivities, (("gz", 3), ("gy", 2), ("gx", 1)), 1)
    mask_x = inside(lax.axis_index("gx"), lax.axis_size("gx"), nx)
    mask_y = inside(lax.axis_index("gy"), lax.axis_size("gy"), ny)
    mask_z = inside(lax.axis_index("gz"), lax.axis_size("gz"), nz)
    valid = mask_x[:, None, None] * mask_y[None, :, None] * mask_z[None, None, :]
    denom = smooth(valid, nx, ny, nz)
    filtered = smooth(padded, nx, ny, nz) / denom[None]
    cells = nx * ny * nz
    dens = density.reshape(-1)
    span = spread.reshape(-1)
    rows = jnp.concatenate(
        [filtered.reshape(FIELDS, cells), jnp.ones((1, cells), jnp.float32)], axis=0
    )
    grow = jnp.maximum(rows, 0.0)
    fall = jnp.maximum(-rows, 0.0)
    square = span * span
    pp = square * (1.001 * grow + 0.001 * fall + RAA)
    qq = square * (0.001 * grow + 1.001 * fall + RAA)
    lower = dens - span
    upper = dens + span
    floor_x = jnp.maximum(0.0, dens - MOVE * span)
    ceil_x = jnp.minimum(1.0, dens + MOVE * span)
    base = (pp[1:] + qq[1:]) / span
    keep = 1.0 - violation
    base_local = jnp.sum(base, axis=1)
    bound = None
    bound = keep * lax.psum(base_local, ("gz", "gy", "gx"))

    def respond(lam):
        weights = jnp.concatenate([jnp.ones((1,), jnp.float32), lam])
        big_p = jnp.dot(weights, pp, precision=lax.Precision.HIGHEST)
        big_q = jnp.dot(weights, qq, precision=lax.Precision.HIGHEST)
        root_p = jnp.sqrt(big_p)
        root_q = jnp.sqrt(big_q)
        moved = (root_p * lower + root_q * upper) / (root_p + root_q)
        return (jnp.clip(moved, floor_x, ceil_x), big_p, big_q)

    lam = multipliers_start
    for step in range(ITERS):
        moved, big_p, big_q = respond(lam)
        above = upper - moved
        below = moved - lower
        values = pp[1:] / above + qq[1:] / below
        slopes = pp[1:] / (above * above) - qq[1:] / (below * below)
        curv = 2.0 * big_p / (above * above * above) + 2.0 * big_q / (below * below * below)
        schur_part = jnp.dot(slopes / curv, slopes.T, precision=lax.Precision.HIGHEST)
        summed, schur = totals(jnp.sum(values, axis=1), schur_part)
        gradient = summed - bound
        shift = REG * jnp.trace(schur) / FIELDS
        system = schur + shift * jnp.eye(FIELDS, dtype=jnp.float32)
        factor = jnp.linalg.cholesky(system)
        delta = jax.scipy.linalg.cho_solve((factor, True), gradient)
        lam = jnp.maximum(lam + delta, FLOOR * lam)
    moved, big_p, big_q = respond(lam)
    return (moved.reshape(nx, ny, nz), lam)


def solution(mesh):
    return jax.shard_map(
        shards,
        mesh=mesh,
        in_specs=(P("gx", "gy", "gz"), P("gx", "gy", "gz"), P(None, "gx", "gy", "gz"), P(), P()),
        out_specs=(P("gx", "gy", "gz"), P()),
        check_vma=False,
    )
```

profile of v0, /device:TPU:0, one launch (start us, length us, event | category | flops | bytes accessed | tf_op | source)
XLA Modules:
  0.0 187.6 jit_solution(5219307162577140861)
XLA Ops:
  0.6 1.5 fusion.136
  2.7 4.9 %collective-permute-start = (f32[9,8,16,1]{2,1,3,0:T(8,128)S(1)}, f32[9,8,16,1]{2,1,3,0:T(8,128)S(1)}, u32[]{:S(2)}, u32[]{:S(2)}) collective-permute-start(f32[9,8,16,1]{2,1,3,0:T(8,128)S(1)} %copy.82), channel_id=1, source_target_pairs={{0,16},{1,17},{2,18},{3,19},{4,20},{5,21},{6,22},{7,23},{8,24},{9,... | collective-permute-start | bytes 13832 | tf_op jit(solution)/shard_map/ppermute | solution.py:21
  8.0 1.3 collective-permute-start.1
  10.5 3.4 %collective-permute-done.1 = f32[9,8,16,1]{2,1,3,0:T(8,128)S(1)} collective-permute-done((f32[9,8,16,1]{2,1,3,0:T(8,128)S(1)}, f32[9,8,16,1]{2,1,3,0:T(8,128)S(1)}, u32[]{:S(2)}, u32[]{:S(2)}) %collective-permute-start.1) | collective-permute-done | bytes 4640 | tf_op jit(solution)/shard_map/ppermute | solution.py:24
  14.5 1.3 collective-permute-start.2
  15.8 1.3 collective-permute-start.3
  17.5 3.2 %collective-permute-done.3 = f32[9,8,1,130]{3,1,2,0:T(8,128)S(1)} collective-permute-done((f32[9,8,1,130]{3,1,2,0:T(8,128)S(1)}, f32[9,8,1,130]{3,1,2,0:T(8,128)S(1)}, u32[]{:S(2)}, u32[]{:S(2)}) %collective-permute-start.3) | collective-permute-done | bytes 37472 | tf_op jit(solution)/shard_map/ppermute | solution.py:24
  20.7 1.0 pad_maximum_fusion.8
  21.7 3.5 %collective-permute-start.4 = (f32[9,1,18,130]{3,2,1,0:T(8,128)S(1)}, f32[9,1,18,130]{3,2,1,0:T(8,128)S(1)}, u32[]{:S(2)}, u32[]{:S(2)}) collective-permute-start(f32[9,1,18,130]{3,2,1,0:T(8,128)S(1)} %copy.60), channel_id=1, source_target_pairs={{0,1},{1,2},{2,3},{4,5},{5,6},{6,7},{8,9},{9,10},{10,11},{12,13},{... | collective-permute-start | bytes 252728 | tf_op jit(solution)/shard_map/ppermute | solution.py:21
  25.3 1.5 collective-permute-start.5
  26.7 1.0 maximum_maximum_fusion.1
  27.7 1.3 collective-permute-done.4
  29.2 4.5 %collective-permute-done.5 = f32[9,1,18,130]{3,2,1,0:T(8,128)S(1)} collective-permute-done((f32[9,1,18,130]{3,2,1,0:T(8,128)S(1)}, f32[9,1,18,130]{3,2,1,0:T(8,128)S(1)}, u32[]{:S(2)}, u32[]{:S(2)}) %collective-permute-start.5) | collective-permute-done | bytes 84272 | tf_op jit(solution)/shard_map/ppermute | solution.py:24
  33.9 2.1 %maximum_maximum_fusion = (f32[9,9,18,130]{3,1,2,0:T(8,128)S(1)}, f32[9,9,18,130]{3,1,2,0:T(8,128)S(1)}) fusion(f32[9,8,1,130]{3,1,2,0:T(8,128)S(1)} %collective-permute-done.3, f32[9,8,16,1]{3,1,2,0:T(8,128)S(1)} %copy.59, f32[9,8,16,128]{3,1,2,0:T(8,128)S(1)} %copy.58, f32[9,8,16,1]{3,1,2,0:T(8,128)S(1)} %copy.57, ...), kind=kLoop, calls=%fused_computation | loop fusion | flops 1895400 | bytes 2358720 | tf_op jit(solution)/shard_map/concatenate | solution.py:25
  36.0 3.1 %fusion.29 = f32[9,8,16,128]{3,1,2,0:T(8,128)S(1)} fusion(f32[9,9,18,130]{3,1,2,0:T(8,128)S(1)} %get-tuple-element.33, f32[9,8,17,130]{3,1,2,0:T(8,128)S(1)} %get-tuple-element.37, f32[9,8,16,1]{3,1,2,0:T(8,128)S(1)} %copy.59, f32[9,8,16,128]{3,1,2,0:T(8,128)S(1)} %copy.58, f32[9,8,16,1]{3,1,2,0:T(8,128)S(1)} %copy.57, ...), kind=kLoop, calls=%fused_computation.47 | loop fusion | flops 8257536 | bytes 15410176 | tf_op jit(solution)/shard_map/div | solution.py:58
  41.9 0.8 fusion.21
  42.8 1.7 fusion.4
  44.5 40.1 %all-reduce.3 = (f32[9,9]{0,1:T(8,128)S(1)}, f32[9]{0:T(128)S(1)}, f32[9]{0:T(128)S(1)}) all-reduce(f32[9,9]{0,1:T(8,128)S(1)} %fusion.4, f32[9]{0:T(128)S(1)} %get-tuple-element.5, f32[9]{0:T(128)S(1)} %get-tuple-element.4), channel_id=1, replica_groups=mesh['gz'=2,'gy'=4,'gx'=4] {'gz','gy','gx'}, use_global_device_ids=true, to_apply=%region_0.0 | all-reduce | flops 99 | bytes 792 | tf_op jit(solution)/shard_map/psum | solution.py:47
  86.0 0.8 cholesky.59
  91.0 1.7 fusion.2
  92.7 40.2 %all-reduce.2 = (f32[9,9]{0,1:T(8,128)S(1)}, f32[9]{0:T(128)S(1)}) all-reduce(f32[9,9]{0,1:T(8,128)S(1)} %fusion.2, f32[9]{0:T(128)S(1)} %add_reduce_fusion.1), channel_id=1, replica_groups=mesh['gz'=2,'gy'=4,'gx'=4] {'gz','gy','gx'}, use_global_device_ids=true, to_apply=%region_8.11 | all-reduce | flops 90 | bytes 720 | tf_op jit(solution)/shard_map/psum | solution.py:47
  134.2 0.8 cholesky.70
  139.3 1.7 fusion
  140.9 40.1 %all-reduce.1 = (f32[9,9]{0,1:T(8,128)S(1)}, f32[9]{0:T(128)S(1)}) all-reduce(f32[9,9]{0,1:T(8,128)S(1)} %fusion, f32[9]{0:T(128)S(1)} %add_reduce_fusion), channel_id=1, replica_groups=mesh['gz'=2,'gy'=4,'gx'=4] {'gz','gy','gx'}, use_global_device_ids=true, to_apply=%region_12.15 | all-reduce | flops 90 | bytes 720 | tf_op jit(solution)/shard_map/psum | solution.py:47
  (89 shorter events, 21.8 us)
Async XLA Ops:
  0.6 9.2 %copy-start = (f32[9,8,16,128]{3,2,1,0:T(8,128)S(1)}, f32[9,8,16,128]{3,2,1,0:T(8,128)}, u32[]{:S(2)}) copy-start(f32[9,8,16,128]{3,2,1,0:T(8,128)} %param.10) | copy-start | bytes 1769476
  2.7 7.4 %collective-permute-start = (f32[9,8,16,1]{2,1,3,0:T(8,128)S(1)}, f32[9,8,16,1]{2,1,3,0:T(8,128)S(1)}, u32[]{:S(2)}, u32[]{:S(2)}) collective-permute-start(f32[9,8,16,1]{2,1,3,0:T(8,128)S(1)} %copy.82), channel_id=1, source_target_pairs={{0,16},{1,17},{2,18},{3,19},{4,20},{5,21},{6,22},{7,23},{8,24},{9,... | collective-permute-start | bytes 13832 | tf_op jit(solution)/shard_map/ppermute | solution.py:21
  8.0 5.9 %collective-permute-start.1 = (f32[9,8,16,1]{2,1,3,0:T(8,128)S(1)}, f32[9,8,16,1]{2,1,3,0:T(8,128)S(1)}, u32[]{:S(2)}, u32[]{:S(2)}) collective-permute-start(f32[9,8,16,1]{2,1,3,0:T(8,128)S(1)} %copy.83), channel_id=1, source_target_pairs={{16,0},{17,1},{18,2},{19,3},{20,4},{21,5},{22,6},{23,7},{24,8},{25... | collective-permute-start | bytes 13832 | tf_op jit(solution)/shard_map/ppermute | solution.py:24
  10.0 7.5 %copy-start.1 = (f32[8,16,128]{2,1,0:T(8,128)S(1)}, f32[8,16,128]{2,1,0:T(8,128)}, u32[]{:S(2)}) copy-start(f32[8,16,128]{2,1,0:T(8,128)} %param.9) | copy-start | bytes 196612
  14.5 3.0 %collective-permute-start.2 = (f32[9,8,1,130]{3,1,2,0:T(8,128)S(1)}, f32[9,8,1,130]{3,1,2,0:T(8,128)S(1)}, u32[]{:S(2)}, u32[]{:S(2)}) collective-permute-start(f32[9,8,1,130]{3,1,2,0:T(8,128)S(1)} %get-tuple-element.38), channel_id=1, source_target_pairs={{0,4},{4,8},{8,12},{1,5},{5,9},{9,13},{2,6},{6,10},{10,14},{3,7},{... | collective-permute-start | bytes 112328 | tf_op jit(solution)/shard_map/ppermute | solution.py:21
  15.8 4.9 %collective-permute-start.3 = (f32[9,8,1,130]{3,1,2,0:T(8,128)S(1)}, f32[9,8,1,130]{3,1,2,0:T(8,128)S(1)}, u32[]{:S(2)}, u32[]{:S(2)}) collective-permute-start(f32[9,8,1,130]{3,1,2,0:T(8,128)S(1)} %get-tuple-element.39), channel_id=1, source_target_pairs={{4,0},{8,4},{12,8},{5,1},{9,5},{13,9},{6,2},{10,6},{14,10},{7,3},{... | collective-permute-start | bytes 112328 | tf_op jit(solution)/shard_map/ppermute | solution.py:24
  21.7 7.3 %collective-permute-start.4 = (f32[9,1,18,130]{3,2,1,0:T(8,128)S(1)}, f32[9,1,18,130]{3,2,1,0:T(8,128)S(1)}, u32[]{:S(2)}, u32[]{:S(2)}) collective-permute-start(f32[9,1,18,130]{3,2,1,0:T(8,128)S(1)} %copy.60), channel_id=1, source_target_pairs={{0,1},{1,2},{2,3},{4,5},{5,6},{6,7},{8,9},{9,10},{10,11},{12,13},{... | collective-permute-start | bytes 252728 | tf_op jit(solution)/shard_map/ppermute | solution.py:21
  25.3 8.4 %collective-permute-start.5 = (f32[9,1,18,130]{3,2,1,0:T(8,128)S(1)}, f32[9,1,18,130]{3,2,1,0:T(8,128)S(1)}, u32[]{:S(2)}, u32[]{:S(2)}) collective-permute-start(f32[9,1,18,130]{3,2,1,0:T(8,128)S(1)} %copy.67), channel_id=1, source_target_pairs={{1,0},{2,1},{3,2},{5,4},{6,5},{7,6},{9,8},{10,9},{11,10},{13,12},{... | collective-permute-start | bytes 252728 | tf_op jit(solution)/shard_map/ppermute | solution.py:24
  39.3 1.2 copy-start.3
  40.0 1.8 copy-start.2
  42.8 46.0 %copy-start.5 = (f32[9]{0:T(128)S(1)}, f32[9]{0:T(128)}, u32[]{:S(2)}) copy-start(f32[9]{0:T(128)} %param.11) | copy-start | bytes 112
  185.6 2.0 %copy-start.4 = (f32[9]{0:T(128)}, f32[9]{0:T(128)S(1)}, u32[]{:S(2)}) copy-start(f32[9]{0:T(128)S(1)} %fusion.11) | copy-start | bytes 112
where the time goes:
time: 188 us
  blocking collectives  120 us (64%)
  other arithmetic  21.8 us (12%)
  starting transfers between devices  13.7 us (7%)
  waiting for transfers between devices  12.4 us (7%)
  matrix products  11 us (6%)
  local copies, waits for them, and re-layouts  5.18 us (3%)
  between operations  3.06 us (2%)
    psum x3, blocking collectives, totals(): return lax.psum((gradient_part, schur_part), ('gz', 'gy', 'gx'))  120 us
    ppermute x3, waiting for transfers between devices, padded_2(): lax.ppermute(lax.slice_in_dim(block, 0, width, axis=dim), axis, backward)  11.1 us
    ppermute x3, starting transfers between devices, padded_2(): lax.ppermute(lax.slice_in_dim(block, block.shape[dim] - width, None, axis...  9.67 us
    dot_general x3, matrix products, shards(): jnp.dot(slopes / curv, slopes.T, precision=lax.Precision.HIGHEST)  5.02 us
    another operation x9, other arithmetic, shards(): factor = jnp.linalg.cholesky(system)  4.45 us
    ppermute x3, starting transfers between devices, padded_2(): lax.ppermute(lax.slice_in_dim(block, 0, width, axis=dim), axis, backward)  4.06 us
    another operation x6, other arithmetic, shards(): delta = jax.scipy.linalg.cho_solve((factor, True), gradient)  4.03 us
  transfers between devices with their start and end apart: 6, of which 4 were waited for; matrix products, arithmetic and copies ran while one was open for 2% of the time, Pallas kernels for 0%

commit v1 on v0

--- a/solution.py
+++ b/solution.py
@@ -44,7 +44,7 @@
 
 
 def totals(gradient_part, schur_part):
-    return lax.psum((gradient_part, schur_part), ("gz", "gy", "gx"))
+    return lax.psum(lax.psum((gradient_part, schur_part), "gz"), ("gy", "gx"))
 
 
 def shards(density, spread, sensitivities, violation, multipliers_start):

time: 188 us -> 219 us (1.16)
  blocking collectives: 120 us -> 151 us
    psum x3 -> x7, blocking collectives: 120 us -> 151 us  [the longest x6 112 us: totals(): return lax.psum(lax.psum((gradient_part, schur_part), 'gz'), ('gy', 'gx'))]
  transfers between devices with their start and end apart: 6 -> 6, of which waited for: 4 -> 4; matrix products, arithmetic and copies ran while one was open for 2% -> 1% of each run, Pallas kernels for 0% -> 0%
where the time goes in v1:
time: 219 us
  blocking collectives  151 us (69%)
  other arithmetic  21.8 us (10%)
  starting transfers between devices  13.7 us (6%)
  waiting for transfers between devices  12.4 us (6%)
  matrix products  11 us (5%)
  local copies, waits for them, and re-layouts  5.18 us (2%)
  between operations  3.08 us (1%)
    psum x6, blocking collectives, totals(): return lax.psum(lax.psum((gradient_part, schur_part), 'gz'), ('gy', 'gx'))  112 us
    psum x1, blocking collectives, shards(): bound = keep * lax.psum(base_local, ('gz', 'gy', 'gx'))  39 us
    ppermute x3, waiting for transfers between devices, padded_2(): lax.ppermute(lax.slice_in_dim(block, 0, width, axis=dim), axis, backward)  11.1 us
    ppermute x3, starting transfers between devices, padded_2(): lax.ppermute(lax.slice_in_dim(block, block.shape[dim] - width, None, axis...  9.67 us
    dot_general x3, matrix products, shards(): jnp.dot(slopes / curv, slopes.T, precision=lax.Precision.HIGHEST)  5.02 us
    another operation x9, other arithmetic, shards(): factor = jnp.linalg.cholesky(system)  4.45 us
  transfers between devices with their start and end apart: 6, of which 4 were waited for; matrix products, arithmetic and copies ran while one was open for 1% of the time, Pallas kernels for 0%

profile of v1, /device:TPU:0, one launch (start us, length us, event | category | flops | bytes accessed | tf_op | source)
XLA Modules:
  0.0 218.5 jit_solution(14672688335127884761)
XLA Ops:
  0.6 1.5 fusion.136
  2.7 4.9 %collective-permute-start = (f32[9,8,16,1]{2,1,3,0:T(8,128)S(1)}, f32[9,8,16,1]{2,1,3,0:T(8,128)S(1)}, u32[]{:S(2)}, u32[]{:S(2)}) collective-permute-start(f32[9,8,16,1]{2,1,3,0:T(8,128)S(1)} %copy.82), channel_id=1, source_target_pairs={{0,16},{1,17},{2,18},{3,19},{4,20},{5,21},{6,22},{7,23},{8,24},{9,... | collective-permute-start | bytes 13832 | tf_op jit(solution)/shard_map/ppermute | solution.py:21
  8.0 1.3 collective-permute-start.1
  10.5 3.4 %collective-permute-done.1 = f32[9,8,16,1]{2,1,3,0:T(8,128)S(1)} collective-permute-done((f32[9,8,16,1]{2,1,3,0:T(8,128)S(1)}, f32[9,8,16,1]{2,1,3,0:T(8,128)S(1)}, u32[]{:S(2)}, u32[]{:S(2)}) %collective-permute-start.1) | collective-permute-done | bytes 4640 | tf_op jit(solution)/shard_map/ppermute | solution.py:24
  14.5 1.3 collective-permute-start.2
  15.8 1.3 collective-permute-start.3
  17.5 3.2 %collective-permute-done.3 = f32[9,8,1,130]{3,1,2,0:T(8,128)S(1)} collective-permute-done((f32[9,8,1,130]{3,1,2,0:T(8,128)S(1)}, f32[9,8,1,130]{3,1,2,0:T(8,128)S(1)}, u32[]{:S(2)}, u32[]{:S(2)}) %collective-permute-start.3) | collective-permute-done | bytes 37472 | tf_op jit(solution)/shard_map/ppermute | solution.py:24
  21.7 3.5 %collective-permute-start.4 = (f32[9,1,18,130]{3,2,1,0:T(8,128)S(1)}, f32[9,1,18,130]{3,2,1,0:T(8,128)S(1)}, u32[]{:S(2)}, u32[]{:S(2)}) collective-permute-start(f32[9,1,18,130]{3,2,1,0:T(8,128)S(1)} %copy.60), channel_id=1, source_target_pairs={{0,1},{1,2},{2,3},{4,5},{5,6},{6,7},{8,9},{9,10},{10,11},{12,13},{... | collective-permute-start | bytes 252728 | tf_op jit(solution)/shard_map/ppermute | solution.py:21
  25.3 1.5 collective-permute-start.5
  26.7 1.0 maximum_maximum_fusion.1
  27.7 1.3 collective-permute-done.4
  29.2 4.5 %collective-permute-done.5 = f32[9,1,18,130]{3,2,1,0:T(8,128)S(1)} collective-permute-done((f32[9,1,18,130]{3,2,1,0:T(8,128)S(1)}, f32[9,1,18,130]{3,2,1,0:T(8,128)S(1)}, u32[]{:S(2)}, u32[]{:S(2)}) %collective-permute-start.5) | collective-permute-done | bytes 84272 | tf_op jit(solution)/shard_map/ppermute | solution.py:24
  33.9 2.1 maximum_maximum_fusion
  36.0 3.1 %fusion.29 = f32[9,8,16,128]{3,1,2,0:T(8,128)S(1)} fusion(f32[9,9,18,130]{3,1,2,0:T(8,128)S(1)} %get-tuple-element.38, f32[9,8,17,130]{3,1,2,0:T(8,128)S(1)} %get-tuple-element.42, f32[9,8,16,1]{3,1,2,0:T(8,128)S(1)} %copy.59, f32[9,8,16,128]{3,1,2,0:T(8,128)S(1)} %copy.58, f32[9,8,16,1]{3,1,2,0:T(8,128)S(1)} %copy.57, ...), kind=kLoop, calls=%fused_computation.47 | loop fusion | flops 8257536 | bytes 15410176 | tf_op jit(solution)/shard_map/div | solution.py:58
  42.8 1.7 fusion.4
  44.5 5.0 %all-reduce.6 = (f32[9,9]{0,1:T(8,128)S(1)}, f32[9]{0:T(128)S(1)}) all-reduce(f32[9,9]{0,1:T(8,128)S(1)} %fusion.4, f32[9]{0:T(128)S(1)} %get-tuple-element.5), channel_id=1, replica_groups=mesh['gz'=2,'gy'=4,'gx'=4] {'gz'}, use_global_device_ids=true, to_apply=%region_0.0 | all-reduce | flops 90 | bytes 720 | tf_op jit(solution)/shard_map/psum | solution.py:47
  49.5 32.6 %all-reduce.3 = (f32[9,9]{0,1:T(8,128)S(1)}, f32[9]{0:T(128)S(1)}) all-reduce(f32[9,9]{0,1:T(8,128)S(1)} %get-tuple-element.16, f32[9]{0:T(128)S(1)} %get-tuple-element.17), channel_id=1, replica_groups=mesh['gz'=2,'gy'=4,'gx'=4] {'gy','gx'}, use_global_device_ids=true, to_apply=%region_1.0 | all-reduce | flops 90 | bytes 720 | tf_op jit(solution)/shard_map/psum | solution.py:47
  86.3 39.0 %psum.95 = f32[9]{0:T(128)S(1)} all-reduce(f32[9]{0:T(128)S(1)} %get-tuple-element.4), channel_id=1, replica_groups=mesh['gz'=2,'gy'=4,'gx'=4] {'gz','gy','gx'}, use_global_device_ids=true, to_apply=%region_9.11 | all-reduce | flops 9 | bytes 72 | tf_op jit(solution)/shard_map/psum | solution.py:78
  127.5 1.7 fusion.2
  129.2 5.3 %all-reduce.5 = (f32[9,9]{0,1:T(8,128)S(1)}, f32[9]{0:T(128)S(1)}) all-reduce(f32[9,9]{0,1:T(8,128)S(1)} %fusion.2, f32[9]{0:T(128)S(1)} %add_reduce_fusion.1), channel_id=1, replica_groups=mesh['gz'=2,'gy'=4,'gx'=4] {'gz'}, use_global_device_ids=true, to_apply=%region_10.13 | all-reduce | flops 90 | bytes 720 | tf_op jit(solution)/shard_map/psum | solution.py:47
  134.5 32.3 %all-reduce.2 = (f32[9,9]{0,1:T(8,128)S(1)}, f32[9]{0:T(128)S(1)}) all-reduce(f32[9,9]{0,1:T(8,128)S(1)} %get-tuple-element.14, f32[9]{0:T(128)S(1)} %get-tuple-element.15), channel_id=1, replica_groups=mesh['gz'=2,'gy'=4,'gx'=4] {'gy','gx'}, use_global_device_ids=true, to_apply=%region_11.14 | all-reduce | flops 90 | bytes 720 | tf_op jit(solution)/shard_map/psum | solution.py:47
  173.2 1.7 fusion
  174.9 5.2 %all-reduce.4 = (f32[9,9]{0,1:T(8,128)S(1)}, f32[9]{0:T(128)S(1)}) all-reduce(f32[9,9]{0,1:T(8,128)S(1)} %fusion, f32[9]{0:T(128)S(1)} %add_reduce_fusion), channel_id=1, replica_groups=mesh['gz'=2,'gy'=4,'gx'=4] {'gz'}, use_global_device_ids=true, to_apply=%region_16.19 | all-reduce | flops 90 | bytes 720 | tf_op jit(solution)/shard_map/psum | solution.py:47
  180.1 31.9 %all-reduce.1 = (f32[9,9]{0,1:T(8,128)S(1)}, f32[9]{0:T(128)S(1)}) all-reduce(f32[9,9]{0,1:T(8,128)S(1)} %get-tuple-element.12, f32[9]{0:T(128)S(1)} %get-tuple-element.13), channel_id=1, replica_groups=mesh['gz'=2,'gy'=4,'gx'=4] {'gy','gx'}, use_global_device_ids=true, to_apply=%region_17.20 | all-reduce | flops 90 | bytes 720 | tf_op jit(solution)/shard_map/psum | solution.py:47
  (93 shorter events, 25.2 us)
Async XLA Ops:
  0.6 9.2 %copy-start = (f32[9,8,16,128]{3,2,1,0:T(8,128)S(1)}, f32[9,8,16,128]{3,2,1,0:T(8,128)}, u32[]{:S(2)}) copy-start(f32[9,8,16,128]{3,2,1,0:T(8,128)} %param.10) | copy-start | bytes 1769476
  2.7 7.4 %collective-permute-start = (f32[9,8,16,1]{2,1,3,0:T(8,128)S(1)}, f32[9,8,16,1]{2,1,3,0:T(8,128)S(1)}, u32[]{:S(2)}, u32[]{:S(2)}) collective-permute-start(f32[9,8,16,1]{2,1,3,0:T(8,128)S(1)} %copy.82), channel_id=1, source_target_pairs={{0,16},{1,17},{2,18},{3,19},{4,20},{5,21},{6,22},{7,23},{8,24},{9,... | collective-permute-start | bytes 13832 | tf_op jit(solution)/shard_map/ppermute | solution.py:21
  8.0 5.9 %collective-permute-start.1 = (f32[9,8,16,1]{2,1,3,0:T(8,128)S(1)}, f32[9,8,16,1]{2,1,3,0:T(8,128)S(1)}, u32[]{:S(2)}, u32[]{:S(2)}) collective-permute-start(f32[9,8,16,1]{2,1,3,0:T(8,128)S(1)} %copy.83), channel_id=1, source_target_pairs={{16,0},{17,1},{18,2},{19,3},{20,4},{21,5},{22,6},{23,7},{24,8},{25... | collective-permute-start | bytes 13832 | tf_op jit(solution)/shard_map/ppermute | solution.py:24
  10.0 7.5 %copy-start.1 = (f32[8,16,128]{2,1,0:T(8,128)S(1)}, f32[8,16,128]{2,1,0:T(8,128)}, u32[]{:S(2)}) copy-start(f32[8,16,128]{2,1,0:T(8,128)} %param.9) | copy-start | bytes 196612
  14.5 3.0 %collective-permute-start.2 = (f32[9,8,1,130]{3,1,2,0:T(8,128)S(1)}, f32[9,8,1,130]{3,1,2,0:T(8,128)S(1)}, u32[]{:S(2)}, u32[]{:S(2)}) collective-permute-start(f32[9,8,1,130]{3,1,2,0:T(8,128)S(1)} %get-tuple-element.43), channel_id=1, source_target_pairs={{0,4},{4,8},{8,12},{1,5},{5,9},{9,13},{2,6},{6,10},{10,14},{3,7},{... | collective-permute-start | bytes 112328 | tf_op jit(solution)/shard_map/ppermute | solution.py:21
  15.8 4.9 %collective-permute-start.3 = (f32[9,8,1,130]{3,1,2,0:T(8,128)S(1)}, f32[9,8,1,130]{3,1,2,0:T(8,128)S(1)}, u32[]{:S(2)}, u32[]{:S(2)}) collective-permute-start(f32[9,8,1,130]{3,1,2,0:T(8,128)S(1)} %get-tuple-element.44), channel_id=1, source_target_pairs={{4,0},{8,4},{12,8},{5,1},{9,5},{13,9},{6,2},{10,6},{14,10},{7,3},{... | collective-permute-start | bytes 112328 | tf_op jit(solution)/shard_map/ppermute | solution.py:24
  21.7 7.3 %collective-permute-start.4 = (f32[9,1,18,130]{3,2,1,0:T(8,128)S(1)}, f32[9,1,18,130]{3,2,1,0:T(8,128)S(1)}, u32[]{:S(2)}, u32[]{:S(2)}) collective-permute-start(f32[9,1,18,130]{3,2,1,0:T(8,128)S(1)} %copy.60), channel_id=1, source_target_pairs={{0,1},{1,2},{2,3},{4,5},{5,6},{6,7},{8,9},{9,10},{10,11},{12,13},{... | collective-permute-start | bytes 252728 | tf_op jit(solution)/shard_map/ppermute | solution.py:21
  25.3 8.4 %collective-permute-start.5 = (f32[9,1,18,130]{3,2,1,0:T(8,128)S(1)}, f32[9,1,18,130]{3,2,1,0:T(8,128)S(1)}, u32[]{:S(2)}, u32[]{:S(2)}) collective-permute-start(f32[9,1,18,130]{3,2,1,0:T(8,128)S(1)} %copy.67), channel_id=1, source_target_pairs={{1,0},{2,1},{3,2},{5,4},{6,5},{7,6},{9,8},{10,9},{11,10},{13,12},{... | collective-permute-start | bytes 252728 | tf_op jit(solution)/shard_map/ppermute | solution.py:24
  39.3 1.2 copy-start.3
  40.0 1.8 copy-start.2
  42.8 82.5 %copy-start.5 = (f32[9]{0:T(128)S(1)}, f32[9]{0:T(128)}, u32[]{:S(2)}) copy-start(f32[9]{0:T(128)} %param.11) | copy-start | bytes 112
  216.5 2.0 copy-start.4
